TPU v7x, 32 devices: a whole 2x2x4 slice. The times are simulated.
32 devices in a mesh: dom: 32 (over z, y, x, core).
Axes of the slice: x: 2, y: 2, z: 4, core: 2. Of those that a mesh axis runs over, the one named last changes fastest.
Arguments:
- features: bfloat16 [32768, 512], P('dom'), may hold values from -6 to 6
- embeddings: bfloat16 [32768, 128], P('dom'), may hold values from -6 to 6
- tile_values: bfloat16 [256, 4, 128, 128], P('dom'), may hold values from -4 to 4
- tile_columns: int32 [256, 4], P('dom'), may hold values from 0 to 11
- send_blocks: int32 [32, 2, 2], P('dom'), may hold values from 0 to 7
- send_count: int32 [32, 2], P('dom'), may hold values from 1 to 2, as said below
- hub_rows: int32 [64], P('dom'), may hold values from 0 to 1023, as said below
- hub_weight: bfloat16 [32768, 64], P('dom'), may hold values from -4 to 4
- degree: int32 [32768], P('dom'), may hold values from 16 to 64
Outputs:
- hop_features: bfloat16 [3, 32768, 512], P(None, 'dom')
- hop_embeddings: bfloat16 [3, 32768, 128], P(None, 'dom')
Inputs may be any that keep to these rules, and one draw needn't show every extreme that they name: `send_count`: some partition sends 2 blocks to its right and some to its left. `hub_rows`: the 2 hub rows of each partition are distinct local row numbers.
All inputs are finite; a program needn't handle non-finite values.
Results may differ from a plain program's by a relative error of at most 0.012.
Values may be sent and summed in bfloat16 or wider, within the bound.
A program may use at most 64 MiB of HBM per device.

v0:
```python
import functools

import jax
import jax.numpy as jnp
from jax import lax
from jax.experimental import pallas as pl
from jax.experimental.pallas import tpu as pltpu
from jax.sharding import PartitionSpec as P

HOPS = 3
LANES = 128
WIDTH = 256
UNROLL = 4
VMEM = 67043328
MESH = pl.DeviceIdType.MESH


def cut(which, columns):
    return [(which, at, min(WIDTH, columns - at)) for at in range(0, columns, WIDTH)]


def kernel(
    n, sizes, cols_ref, listed_ref, count_ref, hubs_ref,
    features_hbm, embeddings_hbm, tiles_hbm, weight_hbm, degree_hbm,
    out_f, out_e, *scratch,
):
    blocks, tile, taps, send_most, hub_dev, pieces = sizes
    chunks = len(pieces)
    per = tile // 16
    pairs = HOPS * chunks
    scratch = list(scratch)
    take = lambda count: [scratch.pop(0) for _ in range(count)]
    locals_, groups, exts, sends, hub_sends, hub_bufs = (take(pairs) for _ in range(6))
    features, embeddings, tiles, weight_t, degree, weight, inv, load_sem, rim_send_sem, rim_recv_sem, hub_send_sem, hub_recv_sem = scratch
    me = lax.axis_index("dom")

    loads = [
        pltpu.make_async_copy(source, held, load_sem.at[q])
        for q, (source, held) in enumerate(
            (
                (degree_hbm, degree),
                (features_hbm, features),
                (embeddings_hbm, embeddings),
                (tiles_hbm, tiles),
                (weight_hbm, weight_t),
            )
        )
    ]
    for load in loads:
        load.start()

    barrier = pltpu.get_barrier_semaphore()

    def greet(step, carry):
        pl.semaphore_signal(
            barrier, inc=1, device_id=(lax.rem(me + step, n),), device_id_type=MESH
        )
        return carry

    lax.fori_loop(1, n, greet, 0)

    loads[0].wait()
    roots = lax.rsqrt(degree[...].astype(jnp.float32)).T
    for b in range(blocks):
        inv[b] = jnp.broadcast_to(roots[:, b : b + 1], (tile, LANES))

    def wide(b, width):
        return jnp.concatenate([inv[b]] * (width // LANES), axis=1)

    @pl.when(me == 0)
    def _():
        for i in range(pairs):
            exts[i][blocks : blocks + send_most] = jnp.zeros((send_most,) + exts[i].shape[1:], jnp.bfloat16)

    @pl.when(me == n - 1)
    def _():
        for i in range(pairs):
            exts[i][blocks + send_most :] = jnp.zeros((send_most,) + exts[i].shape[1:], jnp.bfloat16)

    def rim_copy(i, side):
        first = blocks if side == 1 else blocks + send_most
        to = me + 1 if side == 1 else me - 1
        return pltpu.make_async_remote_copy(
            src_ref=sends[i].at[side],
            dst_ref=exts[i].at[pl.ds(first, send_most)],
            send_sem=rim_send_sem.at[i, side],
            recv_sem=rim_recv_sem.at[i, side],
            device_id=(to,),
            device_id_type=MESH,
        )

    def stage(i):
        source = locals_[i]
        picked = []
        for q in range(hub_dev):
            row = hubs_ref[q]
            near = groups[i][lax.div(row, 16)].astype(jnp.float32)
            here = lax.broadcasted_iota(jnp.int32, near.shape, 0) == lax.rem(row, 16)
            picked.append(jnp.sum(jnp.where(here, near, 0.0), axis=0, keepdims=True))
        packed = jnp.concatenate(picked, axis=0).astype(jnp.bfloat16)
        hub_sends[i][...] = packed
        hub_bufs[i][me] = packed

        for side in range(2):
            for s in range(send_most):
                block = source[listed_ref[0, side, s]]
                keep = jnp.where(s < count_ref[0, side], 1.0, 0.0).astype(jnp.float32)
                sends[i][side, s] = (block.astype(jnp.float32) * keep).astype(jnp.bfloat16)


    def launch(i):
        def spread(step, carry):
            pltpu.make_async_remote_copy(
                src_ref=hub_sends[i],
                dst_ref=hub_bufs[i].at[me],
                send_sem=hub_send_sem.at[i],
                recv_sem=hub_recv_sem.at[i],
                device_id=(lax.rem(me + step, n),),
                device_id_type=MESH,
            ).start()
            return carry

        lax.fori_loop(1, n, spread, 0)

        @pl.when(me < n - 1)
        def _():
            rim_copy(i, 1).start()

        @pl.when(me > 0)
        def _():
            rim_copy(i, 0).start()

    def prepare(c):
        which, at, width = pieces[c]

        def one(b, carry):
            rows = pl.ds(pl.multiple_of(b * tile, tile), tile)
            x = (features, embeddings)[which][rows, at : at + width]
            z = (x.astype(jnp.float32) * wide(b, width)).astype(jnp.bfloat16)
            locals_[c][b] = z
            groups[c][pl.ds(b * per, per)] = z.reshape(per, 16, width)
            exts[c][b] = z
            return carry

        lax.fori_loop(0, blocks, one, 0, unroll=UNROLL)

    loads[1].wait()
    loads[2].wait()
    for c in range(chunks):
        prepare(c)
        stage(c)
    pl.semaphore_wait(barrier, n - 1)
    for c in range(chunks):
        launch(c)

    loads[3].wait()
    loads[4].wait()
    weight[...] = weight_t[...].T

    def drain(i, sem):
        some = hub_bufs[i].at[pl.ds(0, n - 1)]
        pltpu.make_async_copy(some, some, sem.at[i]).wait()

    for hop in range(HOPS):
        for c in range(chunks):
            i = hop * chunks + c
            j = i + chunks
            which, at, width = pieces[c]
            drain(i, hub_recv_sem)

            @pl.when(me > 0)
            def _():
                rim_copy(i, 1).wait_recv()

            @pl.when(me < n - 1)
            def _():
                rim_copy(i, 0).wait_recv()

            hubs = hub_bufs[i][...].reshape(n * hub_dev, width)

            def one(b, carry):
                rows = pl.ds(pl.multiple_of(b * tile, tile), tile)
                left = jnp.concatenate([tiles[b, k] for k in range(taps)], axis=1)
                right = jnp.concatenate(
                    [exts[i][cols_ref[k, b]] for k in range(taps)], axis=0
                )
                y = jnp.dot(left, right, preferred_element_type=jnp.float32)
                y = y + jnp.dot(weight[rows, :], hubs, preferred_element_type=jnp.float32)
                root = wide(b, width)
                x = (y * root).astype(jnp.bfloat16)
                (out_f, out_e)[which][hop, rows, at : at + width] = x
                if hop + 1 < HOPS:
                    z = (x.astype(jnp.float32) * root).astype(jnp.bfloat16)
                    locals_[j][b] = z
                    groups[j][pl.ds(b * per, per)] = z.reshape(per, 16, width)
                    exts[j][b] = z
                return carry

            lax.fori_loop(0, blocks, one, 0, unroll=UNROLL)
            if hop + 1 < HOPS:
                stage(j)
                launch(j)

    for i in range(pairs):
        drain(i, hub_send_sem)

        @pl.when(me < n - 1)
        def _():
            rim_copy(i, 1).wait_send()

        @pl.when(me > 0)
        def _():
            rim_copy(i, 0).wait_send()


def flush(held_f, held_e, out_f, out_e, sem):
    copies = [
        pltpu.make_async_copy(held_f, out_f, sem.at[0]),
        pltpu.make_async_copy(held_e, out_e, sem.at[1]),
    ]
    for copy in copies:
        copy.start()
    for copy in copies:
        copy.wait()


def body(
    features, embeddings, tile_values, tile_columns, send_blocks, send_count,
    hub_rows, hub_weight, degree,
):
    n = lax.axis_size("dom")
    rows = features.shape[0]
    blocks, taps, tile, _ = tile_values.shape
    send_most = send_blocks.shape[2]
    hub_dev = hub_rows.shape[0]
    pieces = cut(0, features.shape[1]) + cut(1, embeddings.shape[1])
    sizes = (blocks, tile, taps, send_most, hub_dev, pieces)
    widths = [width for _, _, width in pieces] * HOPS
    out_bytes = HOPS * rows * (features.shape[1] + embeddings.shape[1]) * 2
    smem = pl.BlockSpec(memory_space=pltpu.SMEM)
    vmem = pl.BlockSpec(memory_space=pltpu.VMEM)
    bf16 = jnp.bfloat16
    held = pl.pallas_call(
        functools.partial(kernel, n, sizes),
        out_shape=(
            pltpu.VMEM((HOPS, rows, features.shape[1]), bf16),
            pltpu.VMEM((HOPS, rows, embeddings.shape[1]), bf16),
        ),
        in_specs=[smem] * 4 + [pl.BlockSpec(memory_space=pltpu.HBM)] * 5,
        out_specs=(vmem, vmem),
        scratch_shapes=[
            pltpu.VMEM(shape + (width,), bf16)
            for shape in (
                (blocks, tile),
                (rows // 16, 16),
                (blocks + 2 * send_most, tile),
                (2, send_most, tile),
                (hub_dev,),
                (n, hub_dev),
            )
            for width in widths
        ]
        + [
            pltpu.VMEM(features.shape, bf16),
            pltpu.VMEM(embeddings.shape, bf16),
            pltpu.VMEM(tile_values.shape, bf16),
            pltpu.VMEM((n * hub_dev, rows), bf16),
            pltpu.VMEM((blocks, tile), jnp.int32),
            pltpu.VMEM((rows, n * hub_dev), bf16),
            pltpu.VMEM((blocks, tile, LANES), jnp.float32),
            pltpu.SemaphoreType.DMA((5,)),
            pltpu.SemaphoreType.DMA((len(widths), 2)),
            pltpu.SemaphoreType.DMA((len(widths), 2)),
            pltpu.SemaphoreType.DMA((len(widths),)),
            pltpu.SemaphoreType.DMA((len(widths),)),
        ],
        compiler_params=pltpu.CompilerParams(
            collective_id=0, has_side_effects=True, vmem_limit_bytes=VMEM - out_bytes
        ),
    )(
        tile_columns.T, send_blocks, send_count, hub_rows,
        features, embeddings, tile_values, hub_weight.T,
        degree.reshape(blocks, tile),
    )
    hbm = pl.BlockSpec(memory_space=pltpu.HBM)
    return pl.pallas_call(
        flush,
        out_shape=tuple(jax.ShapeDtypeStruct(h.shape, h.dtype) for h in held),
        in_specs=[vmem] * 2,
        out_specs=(hbm, hbm),
        scratch_shapes=[pltpu.SemaphoreType.DMA((2,))],
        compiler_params=pltpu.CompilerParams(vmem_limit_bytes=2**20),
    )(*held)


def solution(mesh):
    placed = (
        P("dom", None),
        P("dom", None),
        P("dom", None, None, None),
        P("dom", None),
        P("dom", None, None),
        P("dom", None),
        P("dom"),
        P("dom", None),
        P("dom"),
    )
    return jax.shard_map(
        body,
        mesh=mesh,
        in_specs=placed,
        out_specs=(P(None, "dom", None), P(None, "dom", None)),
        check_vma=False,
    )
```

profile of v0, /device:TPU:0, one launch (start us, length us, event | category | flops | bytes accessed | tf_op | source)
XLA Modules:
  0.0 36.4 jit_solution(827830104275543946)
XLA Ops:
  0.6 33.8 %shard_map.104 = (bf16[3,1024,512]{2,1,0:T(8,128)(2,1)S(1)}, bf16[3,1024,128]{2,1,0:T(8,128)(2,1)S(1)}) custom-call(s32[4,8]{1,0:T(4,128)} %bitcast.5, s32[1,2,2]{2,1,0:T(2,128)} %listed_ref.1, s32[1,2]{1,0:T(1,128)} %count_ref.1, s32[2]{0:T(128)} %hubs_ref.1, bf16[1024,512]{1,0:T(8,128)(2,1)} %features_hbm.1, bf16[1024,128]{1,0:T(8,128)(2,1)} %embeddings_hbm.1, ...), custom_call_target="tpu_custom_call" | custom-call | tf_op jit(solution)/shard_map/pallas_call | solution.py:243
  34.5 1.9 %shard_map.105 = (bf16[3,1024,512]{2,1,0:T(8,128)(2,1)}, bf16[3,1024,128]{2,1,0:T(8,128)(2,1)}) custom-call(bf16[3,1024,512]{2,1,0:T(8,128)(2,1)S(1)} %get-tuple-element.4.held_f, bf16[3,1024,128]{2,1,0:T(8,128)(2,1)S(1)} %get-tuple-element.5.held_e), custom_call_target="tpu_custom_call" | custom-call | tf_op jit(solution)/shard_map/pallas_call | solution.py:286
where the time goes:
time: 36.7 us; the launch traced here: 36.4 us
  Pallas kernels  35.8 us (98%)
  between operations  0.64 us (2%)
    pallas_call x1, Pallas kernels, body(): pl.pallas_call(functools.partial(kernel, n, sizes), out_shape=(pltpu.VMEM...  33.8 us
    pallas_call x1, Pallas kernels, body(): pl.pallas_call(flush, out_shape=tuple((jax.ShapeDtypeStruct(h.shape, h.dt...  1.93 us

commit v1 on v0

--- a/solution.py
+++ b/solution.py
@@ -20,18 +20,23 @@
 
 
 def kernel(
-    n, sizes, cols_ref, listed_ref, count_ref, hubs_ref,
+    n, sizes, cols_hbm, listed_hbm, count_hbm, hubs_hbm,
     features_hbm, embeddings_hbm, tiles_hbm, weight_hbm, degree_hbm,
     out_f, out_e, *scratch,
 ):
-    blocks, tile, taps, send_most, hub_dev, pieces = sizes
+    blocks, tile, taps, send_most, hub_dev, pieces, plane = sizes
+    planes = n // plane
     chunks = len(pieces)
     per = tile // 16
     pairs = HOPS * chunks
     scratch = list(scratch)
     take = lambda count: [scratch.pop(0) for _ in range(count)]
     locals_, groups, exts, sends, hub_sends, hub_bufs = (take(pairs) for _ in range(6))
-    features, embeddings, tiles, weight_t, degree, weight, inv, load_sem, rim_send_sem, rim_recv_sem, hub_send_sem, hub_recv_sem = scratch
+    (
+        cols_ref, listed_ref, count_ref, hubs_ref,
+        features, embeddings, tiles, weight_t, degree, weight, inv,
+        load_sem, rim_send_sem, rim_recv_sem, hub_send_sem, hub_recv_sem, ready,
+    ) = scratch
     me = lax.axis_index("dom")
 
     loads = [
@@ -43,21 +48,47 @@
                 (embeddings_hbm, embeddings),
                 (tiles_hbm, tiles),
                 (weight_hbm, weight_t),
+                (cols_hbm, cols_ref),
+                (listed_hbm, listed_ref),
+                (count_hbm, count_ref),
+                (hubs_hbm, hubs_ref),
             )
         )
     ]
-    for load in loads:
-        load.start()
+    for q in (0, 1, 6, 7, 8, 2, 3, 4, 5):
+        loads[q].start()
 
     barrier = pltpu.get_barrier_semaphore()
+    spot = lax.rem(me, plane)
+    base = me - spot
+    first_in = jnp.logical_and(spot == 0, me > 0)
+    last_in = jnp.logical_and(spot == plane - 1, me < n - 1)
+
+    def call(sem, to):
+        pl.semaphore_signal(sem, inc=1, device_id=(to,), device_id_type=MESH)
+
+    def across(sem):
+        def one(step, carry):
+            call(sem, lax.rem(me + step * plane, n))
+            return carry
+
+        lax.fori_loop(1, planes, one, 0)
 
     def greet(step, carry):
-        pl.semaphore_signal(
-            barrier, inc=1, device_id=(lax.rem(me + step, n),), device_id_type=MESH
-        )
+        call(barrier, base + lax.rem(spot + step, plane))
         return carry
 
-    lax.fori_loop(1, n, greet, 0)
+    across(barrier)
+
+    @pl.when(first_in)
+    def _():
+        call(barrier, me - 1)
+
+    @pl.when(last_in)
+    def _():
+        call(barrier, me + 1)
+
+    lax.fori_loop(1, plane, greet, 0)
 
     loads[0].wait()
     roots = lax.rsqrt(degree[...].astype(jnp.float32)).T
@@ -108,7 +139,7 @@
                 sends[i][side, s] = (block.astype(jnp.float32) * keep).astype(jnp.bfloat16)
 
 
-    def launch(i):
+    def launch_hubs(i):
         def spread(step, carry):
             pltpu.make_async_remote_copy(
                 src_ref=hub_sends[i],
@@ -122,6 +153,7 @@
 
         lax.fori_loop(1, n, spread, 0)
 
+    def launch_rims(i):
         @pl.when(me < n - 1)
         def _():
             rim_copy(i, 1).start()
@@ -144,18 +176,31 @@
 
         lax.fori_loop(0, blocks, one, 0, unroll=UNROLL)
 
-    loads[1].wait()
-    loads[2].wait()
-    for c in range(chunks):
-        prepare(c)
-        stage(c)
-    pl.semaphore_wait(barrier, n - 1)
-    for c in range(chunks):
-        launch(c)
-
-    loads[3].wait()
-    loads[4].wait()
-    weight[...] = weight_t[...].T
+    more = first_in.astype(jnp.int32) + last_in.astype(jnp.int32)
+    with jax.named_scope("group"):
+        pl.semaphore_wait(barrier, planes + plane - 2 + more)
+    across(ready)
+    with jax.named_scope("loads"):
+        for q in (6, 7, 8, 1, 2):
+            loads[q].wait()
+    with jax.named_scope("prepare"):
+        prepare(0)
+        stage(0)
+        launch_rims(0)
+        for c in range(1, chunks):
+            prepare(c)
+            stage(c)
+        loads[3].wait()
+        loads[4].wait()
+        loads[5].wait()
+        weight[...] = weight_t[...].T
+    with jax.named_scope("ready"):
+        pl.semaphore_wait(ready, planes - 1)
+    with jax.named_scope("launch"):
+        for c in range(chunks):
+            launch_hubs(c)
+        for c in range(1, chunks):
+            launch_rims(c)
 
     def drain(i, sem):
         some = hub_bufs[i].at[pl.ds(0, n - 1)]
@@ -166,15 +211,17 @@
             i = hop * chunks + c
             j = i + chunks
             which, at, width = pieces[c]
-            drain(i, hub_recv_sem)
-
-            @pl.when(me > 0)
-            def _():
-                rim_copy(i, 1).wait_recv()
-
-            @pl.when(me < n - 1)
-            def _():
-                rim_copy(i, 0).wait_recv()
+            with jax.named_scope(f"hubwait_{hop}_{c}"):
+                drain(i, hub_recv_sem)
+            with jax.named_scope(f"rimwait_{hop}_{c}"):
+
+                @pl.when(me > 0)
+                def _():
+                    rim_copy(i, 1).wait_recv()
+
+                @pl.when(me < n - 1)
+                def _():
+                    rim_copy(i, 0).wait_recv()
 
             hubs = hub_bufs[i][...].reshape(n * hub_dev, width)
 
@@ -196,21 +243,32 @@
                     exts[j][b] = z
                 return carry
 
-            lax.fori_loop(0, blocks, one, 0, unroll=UNROLL)
+            with jax.named_scope(f"compute_{hop}_{c}"):
+                lax.fori_loop(0, blocks, one, 0, unroll=UNROLL)
             if hop + 1 < HOPS:
-                stage(j)
-                launch(j)
-
-    for i in range(pairs):
-        drain(i, hub_send_sem)
-
-        @pl.when(me < n - 1)
-        def _():
-            rim_copy(i, 1).wait_send()
-
-        @pl.when(me > 0)
-        def _():
-            rim_copy(i, 0).wait_send()
+                with jax.named_scope(f"launch_{hop}_{c}"):
+                    stage(j)
+                    launch_hubs(j)
+                    launch_rims(j)
+
+    with jax.named_scope("drain"):
+        for i in range(pairs):
+            drain(i, hub_send_sem)
+
+            @pl.when(me < n - 1)
+            def _():
+                rim_copy(i, 1).wait_send()
+
+            @pl.when(me > 0)
+            def _():
+                rim_copy(i, 0).wait_send()
+
+
+def group_of(n):
+    size = 1
+    while size * size < n:
+        size *= 2
+    return size if n % size == 0 else n
 
 
 def flush(held_f, held_e, out_f, out_e, sem):
@@ -234,10 +292,9 @@
     send_most = send_blocks.shape[2]
     hub_dev = hub_rows.shape[0]
     pieces = cut(0, features.shape[1]) + cut(1, embeddings.shape[1])
-    sizes = (blocks, tile, taps, send_most, hub_dev, pieces)
+    sizes = (blocks, tile, taps, send_most, hub_dev, pieces, group_of(n))
     widths = [width for _, _, width in pieces] * HOPS
     out_bytes = HOPS * rows * (features.shape[1] + embeddings.shape[1]) * 2
-    smem = pl.BlockSpec(memory_space=pltpu.SMEM)
     vmem = pl.BlockSpec(memory_space=pltpu.VMEM)
     bf16 = jnp.bfloat16
     held = pl.pallas_call(
@@ -246,7 +303,7 @@
             pltpu.VMEM((HOPS, rows, features.shape[1]), bf16),
             pltpu.VMEM((HOPS, rows, embeddings.shape[1]), bf16),
         ),
-        in_specs=[smem] * 4 + [pl.BlockSpec(memory_space=pltpu.HBM)] * 5,
+        in_specs=[pl.BlockSpec(memory_space=pltpu.HBM)] * 9,
         out_specs=(vmem, vmem),
         scratch_shapes=[
             pltpu.VMEM(shape + (width,), bf16)
@@ -261,6 +318,10 @@
             for width in widths
         ]
         + [
+            pltpu.SMEM((taps, blocks), jnp.int32),
+            pltpu.SMEM(send_blocks.shape, jnp.int32),
+            pltpu.SMEM(send_count.shape, jnp.int32),
+            pltpu.SMEM(hub_rows.shape, jnp.int32),
             pltpu.VMEM(features.shape, bf16),
             pltpu.VMEM(embeddings.shape, bf16),
             pltpu.VMEM(tile_values.shape, bf16),
@@ -268,11 +329,12 @@
             pltpu.VMEM((blocks, tile), jnp.int32),
             pltpu.VMEM((rows, n * hub_dev), bf16),
             pltpu.VMEM((blocks, tile, LANES), jnp.float32),
-            pltpu.SemaphoreType.DMA((5,)),
+            pltpu.SemaphoreType.DMA((9,)),
             pltpu.SemaphoreType.DMA((len(widths), 2)),
             pltpu.SemaphoreType.DMA((len(widths), 2)),
             pltpu.SemaphoreType.DMA((len(widths),)),
             pltpu.SemaphoreType.DMA((len(widths),)),
+            pltpu.SemaphoreType.REGULAR,
         ],
         compiler_params=pltpu.CompilerParams(
             collective_id=0, has_side_effects=True, vmem_limit_bytes=VMEM - out_bytes

time: 36.7 us -> 37.4 us (1.019)
  Pallas kernels: 35.8 us -> 36.6 us
    pallas_call x1, Pallas kernels: 33.8 us -> 34.7 us  [body(): pl.pallas_call(functools.partial(kernel, n, sizes), out_shape=(pltpu.VMEM...]
where the time goes in v1:
time: 37.4 us; the launch traced here: 37.2 us
  Pallas kernels  36.6 us (98%)
  between operations  0.64 us (2%)
    pallas_call x1, Pallas kernels, body(): pl.pallas_call(functools.partial(kernel, n, sizes), out_shape=(pltpu.VMEM...  34.7 us
    pallas_call x1, Pallas kernels, body(): pl.pallas_call(flush, out_shape=tuple((jax.ShapeDtypeStruct(h.shape, h.dt...  1.93 us

profile of v1, /device:TPU:0, one launch (start us, length us, event | category | flops | bytes accessed | tf_op | source)
XLA Modules:
  0.0 37.2 jit_solution(7803781139708747598)
XLA Ops:
  0.6 34.7 %shard_map.104 = (bf16[3,1024,512]{2,1,0:T(8,128)(2,1)S(1)}, bf16[3,1024,128]{2,1,0:T(8,128)(2,1)S(1)}) custom-call(s32[4,8]{1,0:T(4,128)} %bitcast.5, s32[1,2,2]{2,1,0:T(2,128)} %listed_hbm.1, s32[1,2]{1,0:T(1,128)} %count_hbm.1, s32[2]{0:T(128)} %hubs_hbm.1, bf16[1024,512]{1,0:T(8,128)(2,1)} %features_hbm.1, bf16[1024,128]{1,0:T(8,128)(2,1)} %embeddings_hbm.1, ...), custom_call_target="tpu_custom_call" | custom-call | tf_op jit(solution)/shard_map/pallas_call | solution.py:300
  35.3 1.9 %shard_map.105 = (bf16[3,1024,512]{2,1,0:T(8,128)(2,1)}, bf16[3,1024,128]{2,1,0:T(8,128)(2,1)}) custom-call(bf16[3,1024,512]{2,1,0:T(8,128)(2,1)S(1)} %get-tuple-element.4.held_f, bf16[3,1024,128]{2,1,0:T(8,128)(2,1)S(1)} %get-tuple-element.5.held_e), custom_call_target="tpu_custom_call" | custom-call | tf_op jit(solution)/shard_map/pallas_call | solution.py:348

commit v2 on v1

--- a/solution.py
+++ b/solution.py
@@ -24,8 +24,7 @@
     features_hbm, embeddings_hbm, tiles_hbm, weight_hbm, degree_hbm,
     out_f, out_e, *scratch,
 ):
-    blocks, tile, taps, send_most, hub_dev, pieces, plane = sizes
-    planes = n // plane
+    blocks, tile, taps, send_most, hub_dev, pieces = sizes
     chunks = len(pieces)
     per = tile // 16
     pairs = HOPS * chunks
@@ -35,7 +34,7 @@
     (
         cols_ref, listed_ref, count_ref, hubs_ref,
         features, embeddings, tiles, weight_t, degree, weight, inv,
-        load_sem, rim_send_sem, rim_recv_sem, hub_send_sem, hub_recv_sem, ready,
+        load_sem, rim_send_sem, rim_recv_sem, hub_send_sem, hub_recv_sem,
     ) = scratch
     me = lax.axis_index("dom")
 
@@ -55,40 +54,19 @@
             )
         )
     ]
-    for q in (0, 1, 6, 7, 8, 2, 3, 4, 5):
+    barrier = pltpu.get_barrier_semaphore()
+
+    def greet(step, carry):
+        pl.semaphore_signal(
+            barrier, inc=1, device_id=(lax.rem(me + step, n),), device_id_type=MESH
+        )
+        return carry
+
+    loads[0].start()
+    loads[1].start()
+    lax.fori_loop(1, n, greet, 0)
+    for q in (6, 7, 8, 2, 3, 4, 5):
         loads[q].start()
-
-    barrier = pltpu.get_barrier_semaphore()
-    spot = lax.rem(me, plane)
-    base = me - spot
-    first_in = jnp.logical_and(spot == 0, me > 0)
-    last_in = jnp.logical_and(spot == plane - 1, me < n - 1)
-
-    def call(sem, to):
-        pl.semaphore_signal(sem, inc=1, device_id=(to,), device_id_type=MESH)
-
-    def across(sem):
-        def one(step, carry):
-            call(sem, lax.rem(me + step * plane, n))
-            return carry
-
-        lax.fori_loop(1, planes, one, 0)
-
-    def greet(step, carry):
-        call(barrier, base + lax.rem(spot + step, plane))
-        return carry
-
-    across(barrier)
-
-    @pl.when(first_in)
-    def _():
-        call(barrier, me - 1)
-
-    @pl.when(last_in)
-    def _():
-        call(barrier, me + 1)
-
-    lax.fori_loop(1, plane, greet, 0)
 
     loads[0].wait()
     roots = lax.rsqrt(degree[...].astype(jnp.float32)).T
@@ -176,31 +154,23 @@
 
         lax.fori_loop(0, blocks, one, 0, unroll=UNROLL)
 
-    more = first_in.astype(jnp.int32) + last_in.astype(jnp.int32)
-    with jax.named_scope("group"):
-        pl.semaphore_wait(barrier, planes + plane - 2 + more)
-    across(ready)
-    with jax.named_scope("loads"):
-        for q in (6, 7, 8, 1, 2):
-            loads[q].wait()
+    for q in (6, 7, 8, 1, 2):
+        loads[q].wait()
     with jax.named_scope("prepare"):
-        prepare(0)
-        stage(0)
-        launch_rims(0)
-        for c in range(1, chunks):
+        for c in range(chunks):
             prepare(c)
             stage(c)
-        loads[3].wait()
-        loads[4].wait()
-        loads[5].wait()
-        weight[...] = weight_t[...].T
-    with jax.named_scope("ready"):
-        pl.semaphore_wait(ready, planes - 1)
+    with jax.named_scope("barrier"):
+        pl.semaphore_wait(barrier, n - 1)
     with jax.named_scope("launch"):
         for c in range(chunks):
             launch_hubs(c)
-        for c in range(1, chunks):
             launch_rims(c)
+
+    with jax.named_scope("weights"):
+        for q in (3, 4, 5):
+            loads[q].wait()
+        weight[...] = weight_t[...].T
 
     def drain(i, sem):
         some = hub_bufs[i].at[pl.ds(0, n - 1)]
@@ -264,13 +234,6 @@
                 rim_copy(i, 0).wait_send()
 
 
-def group_of(n):
-    size = 1
-    while size * size < n:
-        size *= 2
-    return size if n % size == 0 else n
-
-
 def flush(held_f, held_e, out_f, out_e, sem):
     copies = [
         pltpu.make_async_copy(held_f, out_f, sem.at[0]),
@@ -292,7 +255,7 @@
     send_most = send_blocks.shape[2]
     hub_dev = hub_rows.shape[0]
     pieces = cut(0, features.shape[1]) + cut(1, embeddings.shape[1])
-    sizes = (blocks, tile, taps, send_most, hub_dev, pieces, group_of(n))
+    sizes = (blocks, tile, taps, send_most, hub_dev, pieces)
     widths = [width for _, _, width in pieces] * HOPS
     out_bytes = HOPS * rows * (features.shape[1] + embeddings.shape[1]) * 2
     vmem = pl.BlockSpec(memory_space=pltpu.VMEM)
@@ -334,7 +297,6 @@
             pltpu.SemaphoreType.DMA((len(widths), 2)),
             pltpu.SemaphoreType.DMA((len(widths),)),
             pltpu.SemaphoreType.DMA((len(widths),)),
-            pltpu.SemaphoreType.REGULAR,
         ],
         compiler_params=pltpu.CompilerParams(
             collective_id=0, has_side_effects=True, vmem_limit_bytes=VMEM - out_bytes

time: 37.4 us -> 36 us (0.963)
  Pallas kernels: 36.6 us -> 35.1 us
    pallas_call x1, Pallas kernels: 34.7 us -> 33.2 us  [body(): pl.pallas_call(functools.partial(kernel, n, sizes), out_shape=(pltpu.VMEM...]
where the time goes in v2:
time: 36 us; the launch traced here: 35.7 us
  Pallas kernels  35.1 us (98%)
  between operations  0.64 us (2%)
    pallas_call x1, Pallas kernels, body(): pl.pallas_call(functools.partial(kernel, n, sizes), out_shape=(pltpu.VMEM...  33.2 us
    pallas_call x1, Pallas kernels, body(): pl.pallas_call(flush, out_shape=tuple((jax.ShapeDtypeStruct(h.shape, h.dt...  1.93 us

profile of v2, /device:TPU:0, one launch (start us, length us, event | category | flops | bytes accessed | tf_op | source)
XLA Modules:
  0.0 35.7 jit_solution(11871314580787117255)
XLA Ops:
  0.6 33.2 %shard_map.104 = (bf16[3,1024,512]{2,1,0:T(8,128)(2,1)S(1)}, bf16[3,1024,128]{2,1,0:T(8,128)(2,1)S(1)}) custom-call(s32[4,8]{1,0:T(4,128)} %bitcast.5, s32[1,2,2]{2,1,0:T(2,128)} %listed_hbm.1, s32[1,2]{1,0:T(1,128)} %count_hbm.1, s32[2]{0:T(128)} %hubs_hbm.1, bf16[1024,512]{1,0:T(8,128)(2,1)} %features_hbm.1, bf16[1024,128]{1,0:T(8,128)(2,1)} %embeddings_hbm.1, ...), custom_call_target="tpu_custom_call" | custom-call | tf_op jit(solution)/shard_map/pallas_call | solution.py:263
  33.8 1.9 %shard_map.105 = (bf16[3,1024,512]{2,1,0:T(8,128)(2,1)}, bf16[3,1024,128]{2,1,0:T(8,128)(2,1)}) custom-call(bf16[3,1024,512]{2,1,0:T(8,128)(2,1)S(1)} %get-tuple-element.4.held_f, bf16[3,1024,128]{2,1,0:T(8,128)(2,1)S(1)} %get-tuple-element.5.held_e), custom_call_target="tpu_custom_call" | custom-call | tf_op jit(solution)/shard_map/pallas_call | solution.py:310

commit v3 on v2

--- a/solution.py
+++ b/solution.py
@@ -38,43 +38,33 @@
     ) = scratch
     me = lax.axis_index("dom")
 
-    loads = [
-        pltpu.make_async_copy(source, held, load_sem.at[q])
-        for q, (source, held) in enumerate(
-            (
-                (degree_hbm, degree),
-                (features_hbm, features),
-                (embeddings_hbm, embeddings),
-                (tiles_hbm, tiles),
-                (weight_hbm, weight_t),
-                (cols_hbm, cols_ref),
-                (listed_hbm, listed_ref),
-                (count_hbm, count_ref),
-                (hubs_hbm, hubs_ref),
-            )
-        )
+    def load(source, held, q):
+        return pltpu.make_async_copy(source, held, load_sem.at[q])
+
+    load_degree = load(degree_hbm, degree, 0)
+    load_features = load(features_hbm, features, 1)
+    load_embeddings = load(embeddings_hbm, embeddings, 2)
+    small = [
+        load(listed_hbm, listed_ref, 3),
+        load(count_hbm, count_ref, 4),
+        load(hubs_hbm, hubs_ref, 5),
     ]
+    late = [
+        load(tiles_hbm, tiles, 0),
+        load(weight_hbm, weight_t, 1),
+        load(cols_hbm, cols_ref, 2),
+    ]
+    for copy in [load_degree, load_features, load_embeddings] + small:
+        copy.start()
+
     barrier = pltpu.get_barrier_semaphore()
 
     def greet(step, carry):
-        pl.semaphore_signal(
-            barrier, inc=1, device_id=(lax.rem(me + step, n),), device_id_type=MESH
-        )
+        to = lax.rem(me + step, n)
+        pl.semaphore_signal(barrier, inc=1, device_id=(to,), device_id_type=MESH)
         return carry
 
-    loads[0].start()
-    loads[1].start()
     lax.fori_loop(1, n, greet, 0)
-    for q in (6, 7, 8, 2, 3, 4, 5):
-        loads[q].start()
-
-    loads[0].wait()
-    roots = lax.rsqrt(degree[...].astype(jnp.float32)).T
-    for b in range(blocks):
-        inv[b] = jnp.broadcast_to(roots[:, b : b + 1], (tile, LANES))
-
-    def wide(b, width):
-        return jnp.concatenate([inv[b]] * (width // LANES), axis=1)
 
     @pl.when(me == 0)
     def _():
@@ -85,6 +75,14 @@
     def _():
         for i in range(pairs):
             exts[i][blocks + send_most :] = jnp.zeros((send_most,) + exts[i].shape[1:], jnp.bfloat16)
+
+    load_degree.wait()
+    roots = lax.rsqrt(degree[...].astype(jnp.float32)).T
+    for b in range(blocks):
+        inv[b] = jnp.broadcast_to(roots[:, b : b + 1], (tile, LANES))
+
+    def wide(root, width):
+        return jnp.concatenate([root] * (width // LANES), axis=1)
 
     def rim_copy(i, side):
         first = blocks if side == 1 else blocks + send_most
@@ -92,38 +90,65 @@
         return pltpu.make_async_remote_copy(
             src_ref=sends[i].at[side],
             dst_ref=exts[i].at[pl.ds(first, send_most)],
-            send_sem=rim_send_sem.at[i, side],
-            recv_sem=rim_recv_sem.at[i, side],
+            send_sem=rim_send_sem.at[i % chunks],
+            recv_sem=rim_recv_sem.at[i % (2 * chunks)],
             device_id=(to,),
             device_id_type=MESH,
         )
 
-    def stage(i):
-        source = locals_[i]
-        picked = []
-        for q in range(hub_dev):
-            row = hubs_ref[q]
-            near = groups[i][lax.div(row, 16)].astype(jnp.float32)
-            here = lax.broadcasted_iota(jnp.int32, near.shape, 0) == lax.rem(row, 16)
-            picked.append(jnp.sum(jnp.where(here, near, 0.0), axis=0, keepdims=True))
+    inner = jnp.logical_and(me > 0, me < n - 1)
+
+    def rim_wait(i, sem):
+        def of(count):
+            some = exts[i].at[pl.ds(blocks, count)]
+            return pltpu.make_async_copy(some, some, sem)
+
+        @pl.when(inner)
+        def _():
+            of(2 * send_most).wait()
+
+        @pl.when(jnp.logical_not(inner))
+        def _():
+            of(send_most).wait()
+
+    def hub_wait(i, sem):
+        some = hub_bufs[i].at[pl.ds(0, n - 1)]
+        pltpu.make_async_copy(some, some, sem).wait()
+
+    def row_of(rows, row):
+        here = lax.broadcasted_iota(jnp.int32, rows.shape, 0) == lax.rem(row, 16)
+        return jnp.sum(jnp.where(here, rows.astype(jnp.float32), 0.0), axis=0, keepdims=True)
+
+    def stage_rims(i):
+        for side in range(2):
+            for s in range(send_most):
+                block = locals_[i][listed_ref[0, side, s]]
+                keep = jnp.where(s < count_ref[0, side], 1.0, 0.0).astype(jnp.float32)
+                sends[i][side, s] = (block.astype(jnp.float32) * keep).astype(jnp.bfloat16)
+
+    def stage_hubs(i):
+        near = [groups[i][lax.div(hubs_ref[q], 16)] for q in range(hub_dev)]
+        picked = [row_of(near[q], hubs_ref[q]) for q in range(hub_dev)]
         packed = jnp.concatenate(picked, axis=0).astype(jnp.bfloat16)
         hub_sends[i][...] = packed
         hub_bufs[i][me] = packed
 
-        for side in range(2):
-            for s in range(send_most):
-                block = source[listed_ref[0, side, s]]
-                keep = jnp.where(s < count_ref[0, side], 1.0, 0.0).astype(jnp.float32)
-                sends[i][side, s] = (block.astype(jnp.float32) * keep).astype(jnp.bfloat16)
-
+    def launch_rims(i):
+        @pl.when(me < n - 1)
+        def _():
+            rim_copy(i, 1).start()
+
+        @pl.when(me > 0)
+        def _():
+            rim_copy(i, 0).start()
 
     def launch_hubs(i):
         def spread(step, carry):
             pltpu.make_async_remote_copy(
                 src_ref=hub_sends[i],
                 dst_ref=hub_bufs[i].at[me],
-                send_sem=hub_send_sem.at[i],
-                recv_sem=hub_recv_sem.at[i],
+                send_sem=hub_send_sem.at[i % chunks],
+                recv_sem=hub_recv_sem.at[i % (2 * chunks)],
                 device_id=(lax.rem(me + step, n),),
                 device_id_type=MESH,
             ).start()
@@ -131,22 +156,13 @@
 
         lax.fori_loop(1, n, spread, 0)
 
-    def launch_rims(i):
-        @pl.when(me < n - 1)
-        def _():
-            rim_copy(i, 1).start()
-
-        @pl.when(me > 0)
-        def _():
-            rim_copy(i, 0).start()
-
     def prepare(c):
         which, at, width = pieces[c]
 
         def one(b, carry):
             rows = pl.ds(pl.multiple_of(b * tile, tile), tile)
             x = (features, embeddings)[which][rows, at : at + width]
-            z = (x.astype(jnp.float32) * wide(b, width)).astype(jnp.bfloat16)
+            z = (x.astype(jnp.float32) * wide(inv[b], width)).astype(jnp.bfloat16)
             locals_[c][b] = z
             groups[c][pl.ds(b * per, per)] = z.reshape(per, 16, width)
             exts[c][b] = z
@@ -154,27 +170,26 @@
 
         lax.fori_loop(0, blocks, one, 0, unroll=UNROLL)
 
-    for q in (6, 7, 8, 1, 2):
-        loads[q].wait()
-    with jax.named_scope("prepare"):
-        for c in range(chunks):
+    for copy in small + [load_features, load_embeddings]:
+        copy.wait()
+    for copy in late:
+        copy.start()
+
+    for c in range(chunks):
+        with jax.named_scope("prepare"):
             prepare(c)
-            stage(c)
-    with jax.named_scope("barrier"):
-        pl.semaphore_wait(barrier, n - 1)
-    with jax.named_scope("launch"):
-        for c in range(chunks):
+            stage_hubs(c)
+            stage_rims(c)
+        if c == 0:
+            with jax.named_scope("barrier"):
+                pl.semaphore_wait(barrier, n - 1)
+        with jax.named_scope("launch"):
             launch_hubs(c)
             launch_rims(c)
-
     with jax.named_scope("weights"):
-        for q in (3, 4, 5):
-            loads[q].wait()
+        for copy in late:
+            copy.wait()
         weight[...] = weight_t[...].T
-
-    def drain(i, sem):
-        some = hub_bufs[i].at[pl.ds(0, n - 1)]
-        pltpu.make_async_copy(some, some, sem.at[i]).wait()
 
     for hop in range(HOPS):
         for c in range(chunks):
@@ -182,16 +197,9 @@
             j = i + chunks
             which, at, width = pieces[c]
             with jax.named_scope(f"hubwait_{hop}_{c}"):
-                drain(i, hub_recv_sem)
+                hub_wait(i, hub_recv_sem.at[i % (2 * chunks)])
             with jax.named_scope(f"rimwait_{hop}_{c}"):
-
-                @pl.when(me > 0)
-                def _():
-                    rim_copy(i, 1).wait_recv()
-
-                @pl.when(me < n - 1)
-                def _():
-                    rim_copy(i, 0).wait_recv()
+                rim_wait(i, rim_recv_sem.at[i % (2 * chunks)])
 
             hubs = hub_bufs[i][...].reshape(n * hub_dev, width)
 
@@ -203,7 +211,7 @@
                 )
                 y = jnp.dot(left, right, preferred_element_type=jnp.float32)
                 y = y + jnp.dot(weight[rows, :], hubs, preferred_element_type=jnp.float32)
-                root = wide(b, width)
+                root = wide(inv[b], width)
                 x = (y * root).astype(jnp.bfloat16)
                 (out_f, out_e)[which][hop, rows, at : at + width] = x
                 if hop + 1 < HOPS:
@@ -217,21 +225,17 @@
                 lax.fori_loop(0, blocks, one, 0, unroll=UNROLL)
             if hop + 1 < HOPS:
                 with jax.named_scope(f"launch_{hop}_{c}"):
-                    stage(j)
+                    stage_hubs(j)
+                    hub_wait(i, hub_send_sem.at[c])
                     launch_hubs(j)
+                    stage_rims(j)
+                    rim_wait(i, rim_send_sem.at[c])
                     launch_rims(j)
 
     with jax.named_scope("drain"):
-        for i in range(pairs):
-            drain(i, hub_send_sem)
-
-            @pl.when(me < n - 1)
-            def _():
-                rim_copy(i, 1).wait_send()
-
-            @pl.when(me > 0)
-            def _():
-                rim_copy(i, 0).wait_send()
+        for i in range(pairs - chunks, pairs):
+            hub_wait(i, hub_send_sem.at[i % chunks])
+            rim_wait(i, rim_send_sem.at[i % chunks])
 
 
 def flush(held_f, held_e, out_f, out_e, sem):
@@ -255,9 +259,10 @@
     send_most = send_blocks.shape[2]
     hub_dev = hub_rows.shape[0]
     pieces = cut(0, features.shape[1]) + cut(1, embeddings.shape[1])
+    columns = features.shape[1] + embeddings.shape[1]
     sizes = (blocks, tile, taps, send_most, hub_dev, pieces)
     widths = [width for _, _, width in pieces] * HOPS
-    out_bytes = HOPS * rows * (features.shape[1] + embeddings.shape[1]) * 2
+    out_bytes = HOPS * rows * columns * 2
     vmem = pl.BlockSpec(memory_space=pltpu.VMEM)
     bf16 = jnp.bfloat16
     held = pl.pallas_call(
@@ -292,11 +297,11 @@
             pltpu.VMEM((blocks, tile), jnp.int32),
             pltpu.VMEM((rows, n * hub_dev), bf16),
             pltpu.VMEM((blocks, tile, LANES), jnp.float32),
-            pltpu.SemaphoreType.DMA((9,)),
-            pltpu.SemaphoreType.DMA((len(widths), 2)),
-            pltpu.SemaphoreType.DMA((len(widths), 2)),
-            pltpu.SemaphoreType.DMA((len(widths),)),
-            pltpu.SemaphoreType.DMA((len(widths),)),
+            pltpu.SemaphoreType.DMA((6,)),
+            pltpu.SemaphoreType.DMA((len(pieces),)),
+            pltpu.SemaphoreType.DMA((2 * len(pieces),)),
+            pltpu.SemaphoreType.DMA((len(pieces),)),
+            pltpu.SemaphoreType.DMA((2 * len(pieces),)),
         ],
         compiler_params=pltpu.CompilerParams(
             collective_id=0, has_side_effects=True, vmem_limit_bytes=VMEM - out_bytes

time: 36 us -> 35.6 us (0.989)
  Pallas kernels: 35.1 us -> 34.7 us
    pallas_call x1, Pallas kernels: 33.2 us -> 32.8 us  [body(): pl.pallas_call(functools.partial(kernel, n, sizes), out_shape=(pltpu.VMEM...]
where the time goes in v3:
time: 35.6 us; the launch traced here: 35.3 us
  Pallas kernels  34.7 us (97%)
  between operations  0.64 us (2%)
    pallas_call x1, Pallas kernels, body(): pl.pallas_call(functools.partial(kernel, n, sizes), out_shape=(pltpu.VMEM...  32.8 us
    pallas_call x1, Pallas kernels, body(): pl.pallas_call(flush, out_shape=tuple((jax.ShapeDtypeStruct(h.shape, h.dt...  1.93 us

profile of v3, /device:TPU:0, one launch (start us, length us, event | category | flops | bytes accessed | tf_op | source)
XLA Modules:
  0.0 35.3 jit_solution(1110288222869825421)
XLA Ops:
  0.6 32.8 %shard_map.104 = (bf16[3,1024,512]{2,1,0:T(8,128)(2,1)S(1)}, bf16[3,1024,128]{2,1,0:T(8,128)(2,1)S(1)}) custom-call(s32[4,8]{1,0:T(4,128)} %bitcast.5, s32[1,2,2]{2,1,0:T(2,128)} %listed_hbm.1, s32[1,2]{1,0:T(1,128)} %count_hbm.1, s32[2]{0:T(128)} %hubs_hbm.1, bf16[1024,512]{1,0:T(8,128)(2,1)} %features_hbm.1, bf16[1024,128]{1,0:T(8,128)(2,1)} %embeddings_hbm.1, ...), custom_call_target="tpu_custom_call" | custom-call | tf_op jit(solution)/shard_map/pallas_call | solution.py:268
  33.4 1.9 %shard_map.105 = (bf16[3,1024,512]{2,1,0:T(8,128)(2,1)}, bf16[3,1024,128]{2,1,0:T(8,128)(2,1)}) custom-call(bf16[3,1024,512]{2,1,0:T(8,128)(2,1)S(1)} %get-tuple-element.4.held_f, bf16[3,1024,128]{2,1,0:T(8,128)(2,1)S(1)} %get-tuple-element.5.held_e), custom_call_target="tpu_custom_call" | custom-call | tf_op jit(solution)/shard_map/pallas_call | solution.py:315

commit v4 on v3

--- a/solution.py
+++ b/solution.py
@@ -34,7 +34,7 @@
     (
         cols_ref, listed_ref, count_ref, hubs_ref,
         features, embeddings, tiles, weight_t, degree, weight, inv,
-        load_sem, rim_send_sem, rim_recv_sem, hub_send_sem, hub_recv_sem,
+        load_sem, rim_send_sem, rim_recv_sem, hub_send_sem, hub_recv_sem, pass_sem,
     ) = scratch
     me = lax.axis_index("dom")
 
@@ -59,9 +59,18 @@
 
     barrier = pltpu.get_barrier_semaphore()
 
+    quarter = n // 4
+    head = me < 2 * quarter
+    third = jnp.logical_and(me >= 2 * quarter, me < 3 * quarter)
+    tail = me >= 3 * quarter
+
     def greet(step, carry):
         to = lax.rem(me + step, n)
-        pl.semaphore_signal(barrier, inc=1, device_id=(to,), device_id_type=MESH)
+
+        @pl.when(jnp.logical_not(jnp.logical_and(tail, to < 2 * quarter)))
+        def _():
+            pl.semaphore_signal(barrier, inc=1, device_id=(to,), device_id_type=MESH)
+
         return carry
 
     lax.fori_loop(1, n, greet, 0)
@@ -111,9 +120,19 @@
         def _():
             of(send_most).wait()
 
-    def hub_wait(i, sem):
-        some = hub_bufs[i].at[pl.ds(0, n - 1)]
+    def hub_wait(i, sem, count=n - 1):
+        some = hub_bufs[i].at[pl.ds(0, count)]
         pltpu.make_async_copy(some, some, sem).wait()
+
+    def hub_copy(i, held, owner, to, recv_sem):
+        return pltpu.make_async_remote_copy(
+            src_ref=held,
+            dst_ref=hub_bufs[i].at[owner],
+            send_sem=hub_send_sem.at[i % chunks],
+            recv_sem=recv_sem,
+            device_id=(to,),
+            device_id_type=MESH,
+        )
 
     def row_of(rows, row):
         here = lax.broadcasted_iota(jnp.int32, rows.shape, 0) == lax.rem(row, 16)
@@ -143,18 +162,65 @@
             rim_copy(i, 0).start()
 
     def launch_hubs(i):
+        recv_sem = hub_recv_sem.at[i % (2 * chunks)]
+
         def spread(step, carry):
-            pltpu.make_async_remote_copy(
-                src_ref=hub_sends[i],
-                dst_ref=hub_bufs[i].at[me],
-                send_sem=hub_send_sem.at[i % chunks],
-                recv_sem=hub_recv_sem.at[i % (2 * chunks)],
-                device_id=(lax.rem(me + step, n),),
-                device_id_type=MESH,
-            ).start()
+            hub_copy(i, hub_sends[i], me, lax.rem(me + step, n), recv_sem).start()
             return carry
 
         lax.fori_loop(1, n, spread, 0)
+
+    def launch_first(c):
+        recv_sem = hub_recv_sem.at[c]
+
+        def spread(step, carry):
+            hub_copy(c, hub_sends[c], me, lax.rem(me + step, n), recv_sem).start()
+            return carry
+
+        @pl.when(head)
+        def _():
+            source = lax.div(me, quarter)
+            passer = me + (2 - source) * quarter
+            hub_copy(c, hub_sends[c], me, passer, pass_sem.at[c, source]).start()
+
+            def near(step, carry):
+                to = lax.rem(me + step, 3 * quarter)
+
+                @pl.when(to != passer)
+                def _():
+                    hub_copy(c, hub_sends[c], me, to, recv_sem).start()
+
+                return carry
+
+            lax.fori_loop(1, 3 * quarter, near, 0)
+
+        @pl.when(jnp.logical_not(head))
+        def _():
+            lax.fori_loop(1, n, spread, 0)
+
+    def pass_on(c, source):
+        owner = me - (2 - source) * quarter
+        hub_wait(c, pass_sem.at[c, source], 1)
+
+        def spread(step, carry):
+            to = 3 * quarter + lax.rem(me + step, quarter)
+            hub_copy(c, hub_bufs[c].at[owner], owner, to, hub_recv_sem.at[c]).start()
+            return carry
+
+        lax.fori_loop(0, quarter, spread, 0)
+
+    def first_wait(c, sem, of_head, of_third):
+        @pl.when(head)
+        def _():
+            hub_wait(c, sem, of_head)
+
+        @pl.when(third)
+        def _():
+            hub_wait(c, sem, of_third)
+
+        @pl.when(tail)
+        def _():
+            hub_wait(c, sem)
 
     def prepare(c):
         which, at, width = pieces[c]
@@ -182,14 +248,21 @@
             stage_rims(c)
         if c == 0:
             with jax.named_scope("barrier"):
-                pl.semaphore_wait(barrier, n - 1)
+                pl.semaphore_wait(barrier, n - 1 - jnp.where(head, quarter, 0))
         with jax.named_scope("launch"):
-            launch_hubs(c)
+            launch_first(c)
             launch_rims(c)
     with jax.named_scope("weights"):
         for copy in late:
             copy.wait()
         weight[...] = weight_t[...].T
+
+    @pl.when(third)
+    def _():
+        with jax.named_scope("pass"):
+            for c in range(chunks):
+                pass_on(c, 1)
+                pass_on(c, 0)
 
     for hop in range(HOPS):
         for c in range(chunks):
@@ -197,11 +270,14 @@
             j = i + chunks
             which, at, width = pieces[c]
             with jax.named_scope(f"hubwait_{hop}_{c}"):
-                hub_wait(i, hub_recv_sem.at[i % (2 * chunks)])
+                if hop:
+                    hub_wait(i, hub_recv_sem.at[i % (2 * chunks)])
+                else:
+                    first_wait(c, hub_recv_sem.at[c], n - 1, n - 3)
             with jax.named_scope(f"rimwait_{hop}_{c}"):
                 rim_wait(i, rim_recv_sem.at[i % (2 * chunks)])
 
-            hubs = hub_bufs[i][...].reshape(n * hub_dev, width)
+            hubs = hub_bufs[i][:n].reshape(n * hub_dev, width)
 
             def one(b, carry):
                 rows = pl.ds(pl.multiple_of(b * tile, tile), tile)
@@ -226,7 +302,10 @@
             if hop + 1 < HOPS:
                 with jax.named_scope(f"launch_{hop}_{c}"):
                     stage_hubs(j)
-                    hub_wait(i, hub_send_sem.at[c])
+                    if hop:
+                        hub_wait(i, hub_send_sem.at[c])
+                    else:
+                        first_wait(c, hub_send_sem.at[c], n - 1 - quarter, n - 1 + 2 * quarter)
                     launch_hubs(j)
                     stage_rims(j)
                     rim_wait(i, rim_send_sem.at[c])
@@ -281,7 +360,7 @@
                 (blocks + 2 * send_most, tile),
                 (2, send_most, tile),
                 (hub_dev,),
-                (n, hub_dev),
+                (n + n // 2, hub_dev),
             )
             for width in widths
         ]
@@ -302,6 +381,7 @@
             pltpu.SemaphoreType.DMA((2 * len(pieces),)),
             pltpu.SemaphoreType.DMA((len(pieces),)),
             pltpu.SemaphoreType.DMA((2 * len(pieces),)),
+            pltpu.SemaphoreType.DMA((len(pieces), 2)),
         ],
         compiler_params=pltpu.CompilerParams(
             collective_id=0, has_side_effects=True, vmem_limit_bytes=VMEM - out_bytes

time: 35.6 us -> 35 us (0.983)
  Pallas kernels: 34.7 us -> 34.1 us
    pallas_call x1, Pallas kernels: 32.8 us -> 32.2 us  [body(): pl.pallas_call(functools.partial(kernel, n, sizes), out_shape=(pltpu.VMEM...]
where the time goes in v4:
time: 35 us; the launch traced here: 34.7 us
  Pallas kernels  34.1 us (97%)
  between operations  0.64 us (2%)
    pallas_call x1, Pallas kernels, body(): pl.pallas_call(functools.partial(kernel, n, sizes), out_shape=(pltpu.VMEM...  32.2 us
    pallas_call x1, Pallas kernels, body(): pl.pallas_call(flush, out_shape=tuple((jax.ShapeDtypeStruct(h.shape, h.dt...  1.93 us

profile of v4, /device:TPU:0, one launch (start us, length us, event | category | flops | bytes accessed | tf_op | source)
XLA Modules:
  0.0 34.7 jit_solution(3926720488147117816)
XLA Ops:
  0.6 32.2 %shard_map.104 = (bf16[3,1024,512]{2,1,0:T(8,128)(2,1)S(1)}, bf16[3,1024,128]{2,1,0:T(8,128)(2,1)S(1)}) custom-call(s32[4,8]{1,0:T(4,128)} %bitcast.5, s32[1,2,2]{2,1,0:T(2,128)} %listed_hbm.1, s32[1,2]{1,0:T(1,128)} %count_hbm.1, s32[2]{0:T(128)} %hubs_hbm.1, bf16[1024,512]{1,0:T(8,128)(2,1)} %features_hbm.1, bf16[1024,128]{1,0:T(8,128)(2,1)} %embeddings_hbm.1, ...), custom_call_target="tpu_custom_call" | custom-call | tf_op jit(solution)/shard_map/pallas_call | solution.py:347
  32.8 1.9 %shard_map.105 = (bf16[3,1024,512]{2,1,0:T(8,128)(2,1)}, bf16[3,1024,128]{2,1,0:T(8,128)(2,1)}) custom-call(bf16[3,1024,512]{2,1,0:T(8,128)(2,1)S(1)} %get-tuple-element.4.held_f, bf16[3,1024,128]{2,1,0:T(8,128)(2,1)S(1)} %get-tuple-element.5.held_e), custom_call_target="tpu_custom_call" | custom-call | tf_op jit(solution)/shard_map/pallas_call | solution.py:395

commit v5 on v4

--- a/solution.py
+++ b/solution.py
@@ -1,4 +1,5 @@
 import functools
+import math
 
 import jax
 import jax.numpy as jnp
@@ -19,10 +20,21 @@
     return [(which, at, min(WIDTH, columns - at)) for at in range(0, columns, WIDTH)]
 
 
+def wide(root, width):
+    return jnp.concatenate([root] * (width // LANES), axis=1)
+
+
+def gathered(b, rows, taps, tiles, weight, cols, ext, hubs):
+    left = jnp.concatenate([tiles[b, k] for k in range(taps)], axis=1)
+    right = jnp.concatenate([ext[cols[k, b]] for k in range(taps)], axis=0)
+    y = jnp.dot(left, right, preferred_element_type=jnp.float32)
+    return y + jnp.dot(weight[rows, :], hubs, preferred_element_type=jnp.float32)
+
+
 def kernel(
     n, sizes, cols_hbm, listed_hbm, count_hbm, hubs_hbm,
     features_hbm, embeddings_hbm, tiles_hbm, weight_hbm, degree_hbm,
-    out_f, out_e, *scratch,
+    out_f, out_e, tiles, weight, inv, last_ext, last_hubs, *scratch,
 ):
     blocks, tile, taps, send_most, hub_dev, pieces = sizes
     chunks = len(pieces)
@@ -30,10 +42,12 @@
     pairs = HOPS * chunks
     scratch = list(scratch)
     take = lambda count: [scratch.pop(0) for _ in range(count)]
-    locals_, groups, exts, sends, hub_sends, hub_bufs = (take(pairs) for _ in range(6))
+    locals_, groups, sends, hub_sends = (take(pairs) for _ in range(4))
+    exts = take(pairs - 1) + [last_ext]
+    hub_bufs = take(pairs - 1) + [last_hubs]
     (
         cols_ref, listed_ref, count_ref, hubs_ref,
-        features, embeddings, tiles, weight_t, degree, weight, inv,
+        features, embeddings, weight_t, degree,
         load_sem, rim_send_sem, rim_recv_sem, hub_send_sem, hub_recv_sem, pass_sem,
     ) = scratch
     me = lax.axis_index("dom")
@@ -90,9 +104,6 @@
     for b in range(blocks):
         inv[b] = jnp.broadcast_to(roots[:, b : b + 1], (tile, LANES))
 
-    def wide(root, width):
-        return jnp.concatenate([root] * (width // LANES), axis=1)
-
     def rim_copy(i, side):
         first = blocks if side == 1 else blocks + send_most
         to = me + 1 if side == 1 else me - 1
@@ -277,16 +288,14 @@
             with jax.named_scope(f"rimwait_{hop}_{c}"):
                 rim_wait(i, rim_recv_sem.at[i % (2 * chunks)])
 
+            if i == pairs - 1:
+                continue
+
             hubs = hub_bufs[i][:n].reshape(n * hub_dev, width)
 
             def one(b, carry):
                 rows = pl.ds(pl.multiple_of(b * tile, tile), tile)
-                left = jnp.concatenate([tiles[b, k] for k in range(taps)], axis=1)
-                right = jnp.concatenate(
-                    [exts[i][cols_ref[k, b]] for k in range(taps)], axis=0
-                )
-                y = jnp.dot(left, right, preferred_element_type=jnp.float32)
-                y = y + jnp.dot(weight[rows, :], hubs, preferred_element_type=jnp.float32)
+                y = gathered(b, rows, taps, tiles, weight, cols_ref, exts[i], hubs)
                 root = wide(inv[b], width)
                 x = (y * root).astype(jnp.bfloat16)
                 (out_f, out_e)[which][hop, rows, at : at + width] = x
@@ -317,14 +326,37 @@
             rim_wait(i, rim_send_sem.at[i % chunks])
 
 
-def flush(held_f, held_e, out_f, out_e, sem):
+def flush(
+    n, sizes, held_f, held_e, tiles, weight, inv, ext, hubs_ref, cols_hbm,
+    out_f, out_e, cols, held, sem,
+):
+    blocks, tile, taps, send_most, hub_dev, pieces = sizes
+    _, at, width = pieces[-1]
+    last = HOPS - 1
+    fetch = pltpu.make_async_copy(cols_hbm, cols, sem.at[0])
+    fetch.start()
     copies = [
-        pltpu.make_async_copy(held_f, out_f, sem.at[0]),
-        pltpu.make_async_copy(held_e, out_e, sem.at[1]),
+        pltpu.make_async_copy(held_f, out_f, sem.at[1]),
+        pltpu.make_async_copy(held_e.at[:last], out_e.at[:last], sem.at[2]),
     ]
+    if at:
+        done = pl.ds(0, at)
+        copies.append(pltpu.make_async_copy(held_e.at[last, :, done], out_e.at[last, :, done], sem.at[3]))
     for copy in copies:
         copy.start()
-    for copy in copies:
+    fetch.wait()
+    hubs = hubs_ref[:n].reshape(n * hub_dev, width)
+
+    def one(b, carry):
+        rows = pl.ds(pl.multiple_of(b * tile, tile), tile)
+        y = gathered(b, rows, taps, tiles, weight, cols, ext, hubs)
+        held[rows, :] = (y * wide(inv[b], width)).astype(jnp.bfloat16)
+        return carry
+
+    lax.fori_loop(0, blocks, one, 0, unroll=UNROLL)
+    rest = pltpu.make_async_copy(held, out_e.at[last, :, pl.ds(at, width)], sem.at[4])
+    rest.start()
+    for copy in copies + [rest]:
         copy.wait()
 
 
@@ -338,31 +370,38 @@
     send_most = send_blocks.shape[2]
     hub_dev = hub_rows.shape[0]
     pieces = cut(0, features.shape[1]) + cut(1, embeddings.shape[1])
-    columns = features.shape[1] + embeddings.shape[1]
     sizes = (blocks, tile, taps, send_most, hub_dev, pieces)
     widths = [width for _, _, width in pieces] * HOPS
-    out_bytes = HOPS * rows * columns * 2
     vmem = pl.BlockSpec(memory_space=pltpu.VMEM)
+    hbm = pl.BlockSpec(memory_space=pltpu.HBM)
     bf16 = jnp.bfloat16
+    results = [
+        ((HOPS, rows, features.shape[1]), bf16),
+        ((HOPS, rows, embeddings.shape[1]), bf16),
+        (tile_values.shape, bf16),
+        ((rows, n * hub_dev), bf16),
+        ((blocks, tile, LANES), jnp.float32),
+        ((blocks + 2 * send_most, tile, widths[-1]), bf16),
+        ((n + n // 2, hub_dev, widths[-1]), bf16),
+    ]
+    out_bytes = sum(math.prod(shape[:-1]) * max(shape[-1], LANES) * jnp.dtype(kind).itemsize for shape, kind in results)
+    columns = tile_columns.T
     held = pl.pallas_call(
         functools.partial(kernel, n, sizes),
-        out_shape=(
-            pltpu.VMEM((HOPS, rows, features.shape[1]), bf16),
-            pltpu.VMEM((HOPS, rows, embeddings.shape[1]), bf16),
-        ),
-        in_specs=[pl.BlockSpec(memory_space=pltpu.HBM)] * 9,
-        out_specs=(vmem, vmem),
+        out_shape=tuple(pltpu.VMEM(shape, kind) for shape, kind in results),
+        in_specs=[hbm] * 9,
+        out_specs=(vmem,) * len(results),
         scratch_shapes=[
             pltpu.VMEM(shape + (width,), bf16)
-            for shape in (
-                (blocks, tile),
-                (rows // 16, 16),
-                (blocks + 2 * send_most, tile),
-                (2, send_most, tile),
-                (hub_dev,),
-                (n + n // 2, hub_dev),
+            for shape, some in (
+                ((blocks, tile), widths),
+                ((rows // 16, 16), widths),
+                ((2, send_most, tile), widths),
+                ((hub_dev,), widths),
+                ((blocks + 2 * send_most, tile), widths[:-1]),
+                ((n + n // 2, hub_dev), widths[:-1]),
             )
-            for width in widths
+            for width in some
         ]
         + [
             pltpu.SMEM((taps, blocks), jnp.int32),
@@ -371,11 +410,8 @@
             pltpu.SMEM(hub_rows.shape, jnp.int32),
             pltpu.VMEM(features.shape, bf16),
             pltpu.VMEM(embeddings.shape, bf16),
-            pltpu.VMEM(tile_values.shape, bf16),
             pltpu.VMEM((n * hub_dev, rows), bf16),
             pltpu.VMEM((blocks, tile), jnp.int32),
-            pltpu.VMEM((rows, n * hub_dev), bf16),
-            pltpu.VMEM((blocks, tile, LANES), jnp.float32),
             pltpu.SemaphoreType.DMA((6,)),
             pltpu.SemaphoreType.DMA((len(pieces),)),
             pltpu.SemaphoreType.DMA((2 * len(pieces),)),
@@ -387,19 +423,22 @@
             collective_id=0, has_side_effects=True, vmem_limit_bytes=VMEM - out_bytes
         ),
     )(
-        tile_columns.T, send_blocks, send_count, hub_rows,
+        columns, send_blocks, send_count, hub_rows,
         features, embeddings, tile_values, hub_weight.T,
         degree.reshape(blocks, tile),
     )
-    hbm = pl.BlockSpec(memory_space=pltpu.HBM)
     return pl.pallas_call(
-        flush,
-        out_shape=tuple(jax.ShapeDtypeStruct(h.shape, h.dtype) for h in held),
-        in_specs=[vmem] * 2,
+        functools.partial(flush, n, sizes),
+        out_shape=tuple(jax.ShapeDtypeStruct(h.shape, h.dtype) for h in held[:2]),
+        in_specs=[vmem] * len(held) + [hbm],
         out_specs=(hbm, hbm),
-        scratch_shapes=[pltpu.SemaphoreType.DMA((2,))],
-        compiler_params=pltpu.CompilerParams(vmem_limit_bytes=2**20),
-    )(*held)
+        scratch_shapes=[
+            pltpu.SMEM((taps, blocks), jnp.int32),
+            pltpu.VMEM((rows, widths[-1]), bf16),
+            pltpu.SemaphoreType.DMA((5,)),
+        ],
+        compiler_params=pltpu.CompilerParams(vmem_limit_bytes=4 * 2**20),
+    )(*held, columns)
 
 
 def solution(mesh):

time: 35 us -> 35.1 us (level)
  local copies, waits for them, and re-layouts: 0 us -> 0.68 us
  Pallas kernels: 34.1 us -> 33.5 us
    unnamed x0 -> x2, local copies, waits for them, and re-layouts: none -> 0.68 us
    pallas_call x2, Pallas kernels: 34.1 us -> 33.5 us  [the longest x1 31.5 us: body(): pl.pallas_call(functools.partial(kernel, n, sizes), out_shape=tuple((pltp...]
where the time goes in v5:
time: 35.1 us; the launch traced here: 34.8 us
  Pallas kernels  33.5 us (95%)
  local copies, waits for them, and re-layouts  0.68 us (2%)
  between operations  0.65 us (2%)
    pallas_call x1, Pallas kernels, body(): pl.pallas_call(functools.partial(kernel, n, sizes), out_shape=tuple((pltp...  31.5 us
    pallas_call x1, Pallas kernels, body(): pl.pallas_call(functools.partial(flush, n, sizes), out_shape=tuple((jax.S...  1.97 us

profile of v5, /device:TPU:0, one launch (start us, length us, event | category | flops | bytes accessed | tf_op | source)
XLA Modules:
  0.0 34.8 jit_solution(17750123177610830691)
XLA Ops:
  0.6 31.5 %shard_map.104 = (bf16[3,1024,512]{2,1,0:T(8,128)(2,1)S(1)}, bf16[3,1024,128]{2,1,0:T(8,128)(2,1)S(1)}, bf16[8,4,128,128]{3,2,1,0:T(8,128)(2,1)S(1)}, bf16[1024,...) custom-call(s32[4,8]{1,0:T(4,128)} %bitcast.3, ...), custom_call_target="tpu_custom_call" | custom-call | tf_op jit(solution)/shard_map/pallas_call | solution.py:389
  32.1 0.0 copy-start
  32.1 0.7 %copy-done = s32[8,4]{0,1:T(4,128)S(1)} copy-done((s32[8,4]{0,1:T(4,128)S(1)}, s32[8,4]{0,1:T(4,128)}, u32[]{:S(2)}) %copy-start) | copy-done | bytes 152
  32.8 2.0 %shard_map.105 = (bf16[3,1024,512]{2,1,0:T(8,128)(2,1)}, bf16[3,1024,128]{2,1,0:T(8,128)(2,1)}) custom-call(bf16[3,1024,512]{2,1,0:T(8,128)(2,1)S(1)} %get-tuple-element.9.held_f, bf16[3,1024,128]{2,1,0:T(8,128)(2,1)S(1)} %get-tuple-element.10.held_e, bf16[8,4,128,128]{3,2,1,0:T(8,128)(2,1)S(1)} %get-tuple-element.11.tiles, ...), custom_call_target="tpu_custom_call" | custom-call | tf_op jit(solution)/shard_map/pallas_call | solution.py:430
Async XLA Ops:
  32.1 0.7 %copy-start = (s32[8,4]{0,1:T(4,128)S(1)}, s32[8,4]{0,1:T(4,128)}, u32[]{:S(2)}) copy-start(s32[8,4]{0,1:T(4,128)} %param.12) | copy-start | bytes 388

commit v6 on v5

--- a/solution.py
+++ b/solution.py
@@ -34,7 +34,7 @@
 def kernel(
     n, sizes, cols_hbm, listed_hbm, count_hbm, hubs_hbm,
     features_hbm, embeddings_hbm, tiles_hbm, weight_hbm, degree_hbm,
-    out_f, out_e, tiles, weight, inv, last_ext, last_hubs, *scratch,
+    out_f, out_e, tiles, weight, inv, last_ext, last_hubs, cols_held, *scratch,
 ):
     blocks, tile, taps, send_most, hub_dev, pieces = sizes
     chunks = len(pieces)
@@ -67,6 +67,7 @@
         load(tiles_hbm, tiles, 0),
         load(weight_hbm, weight_t, 1),
         load(cols_hbm, cols_ref, 2),
+        load(cols_hbm, cols_held, 3),
     ]
     for copy in [load_degree, load_features, load_embeddings] + small:
         copy.start()
@@ -327,13 +328,13 @@
 
 
 def flush(
-    n, sizes, held_f, held_e, tiles, weight, inv, ext, hubs_ref, cols_hbm,
+    n, sizes, held_f, held_e, tiles, weight, inv, ext, hubs_ref, cols_held,
     out_f, out_e, cols, held, sem,
 ):
     blocks, tile, taps, send_most, hub_dev, pieces = sizes
     _, at, width = pieces[-1]
     last = HOPS - 1
-    fetch = pltpu.make_async_copy(cols_hbm, cols, sem.at[0])
+    fetch = pltpu.make_async_copy(cols_held, cols, sem.at[0])
     fetch.start()
     copies = [
         pltpu.make_async_copy(held_f, out_f, sem.at[1]),
@@ -383,9 +384,9 @@
         ((blocks, tile, LANES), jnp.float32),
         ((blocks + 2 * send_most, tile, widths[-1]), bf16),
         ((n + n // 2, hub_dev, widths[-1]), bf16),
+        ((taps, blocks), jnp.int32),
     ]
     out_bytes = sum(math.prod(shape[:-1]) * max(shape[-1], LANES) * jnp.dtype(kind).itemsize for shape, kind in results)
-    columns = tile_columns.T
     held = pl.pallas_call(
         functools.partial(kernel, n, sizes),
         out_shape=tuple(pltpu.VMEM(shape, kind) for shape, kind in results),
@@ -420,17 +421,17 @@
             pltpu.SemaphoreType.DMA((len(pieces), 2)),
         ],
         compiler_params=pltpu.CompilerParams(
-            collective_id=0, has_side_effects=True, vmem_limit_bytes=VMEM - out_bytes
+            collective_id=0, has_side_effects=True, vmem_limit_bytes=VMEM - out_bytes - 2**20
         ),
     )(
-        columns, send_blocks, send_count, hub_rows,
+        tile_columns.T, send_blocks, send_count, hub_rows,
         features, embeddings, tile_values, hub_weight.T,
         degree.reshape(blocks, tile),
     )
     return pl.pallas_call(
         functools.partial(flush, n, sizes),
         out_shape=tuple(jax.ShapeDtypeStruct(h.shape, h.dtype) for h in held[:2]),
-        in_specs=[vmem] * len(held) + [hbm],
+        in_specs=[vmem] * len(held),
         out_specs=(hbm, hbm),
         scratch_shapes=[
             pltpu.SMEM((taps, blocks), jnp.int32),
@@ -438,7 +439,7 @@
             pltpu.SemaphoreType.DMA((5,)),
         ],
         compiler_params=pltpu.CompilerParams(vmem_limit_bytes=4 * 2**20),
-    )(*held, columns)
+    )(*held)
 
 
 def solution(mesh):

time: 35.1 us -> 34.4 us (0.980)
  local copies, waits for them, and re-layouts: 0.68 us -> 0 us
    unnamed x2 -> x0, local copies, waits for them, and re-layouts: 0.68 us -> none
where the time goes in v6:
time: 34.4 us; the launch traced here: 34.1 us
  Pallas kernels  33.5 us (97%)
  between operations  0.64 us (2%)
    pallas_call x1, Pallas kernels, body(): pl.pallas_call(functools.partial(kernel, n, sizes), out_shape=tuple((pltp...  31.5 us
    pallas_call x1, Pallas kernels, body(): pl.pallas_call(functools.partial(flush, n, sizes), out_shape=tuple((jax.S...  1.97 us

profile of v6, /device:TPU:0, one launch (start us, length us, event | category | flops | bytes accessed | tf_op | source)
XLA Modules:
  0.0 34.1 jit_solution(4040358980904419747)
XLA Ops:
  0.6 31.5 %shard_map.104 = (bf16[3,1024,512]{2,1,0:T(8,128)(2,1)S(1)}, bf16[3,1024,128]{2,1,0:T(8,128)(2,1)S(1)}, bf16[8,4,128,128]{3,2,1,0:T(8,128)(2,1)S(1)}, bf16[1024,...) custom-call(s32[4,8]{1,0:T(4,128)} %bitcast.5, ...), custom_call_target="tpu_custom_call" | custom-call | tf_op jit(solution)/shard_map/pallas_call | solution.py:390
  32.1 2.0 %shard_map.105 = (bf16[3,1024,512]{2,1,0:T(8,128)(2,1)}, bf16[3,1024,128]{2,1,0:T(8,128)(2,1)}) custom-call(bf16[3,1024,512]{2,1,0:T(8,128)(2,1)S(1)} %get-tuple-element.10.held_f, bf16[3,1024,128]{2,1,0:T(8,128)(2,1)S(1)} %get-tuple-element.11.held_e, bf16[8,4,128,128]{3,2,1,0:T(8,128)(2,1)S(1)} %get-tuple-element.12.tiles, ...), custom_call_target="tpu_custom_call" | custom-call | tf_op jit(solution)/shard_map/pallas_call | solution.py:431

commit v7 on v6

--- a/solution.py
+++ b/solution.py
@@ -10,7 +10,7 @@
 
 HOPS = 3
 LANES = 128
-WIDTH = 256
+WIDTH = 128
 UNROLL = 4
 VMEM = 67043328
 MESH = pl.DeviceIdType.MESH
@@ -69,7 +69,7 @@
         load(cols_hbm, cols_ref, 2),
         load(cols_hbm, cols_held, 3),
     ]
-    for copy in [load_degree, load_features, load_embeddings] + small:
+    for copy in [load_degree, load_features, load_embeddings]:
         copy.start()
 
     barrier = pltpu.get_barrier_semaphore()
@@ -79,16 +79,16 @@
     third = jnp.logical_and(me >= 2 * quarter, me < 3 * quarter)
     tail = me >= 3 * quarter
 
-    def greet(step, carry):
-        to = lax.rem(me + step, n)
-
-        @pl.when(jnp.logical_not(jnp.logical_and(tail, to < 2 * quarter)))
+    def greet(to, carry):
+        @pl.when(to != me)
         def _():
             pl.semaphore_signal(barrier, inc=1, device_id=(to,), device_id_type=MESH)
 
         return carry
 
-    lax.fori_loop(1, n, greet, 0)
+    lax.fori_loop(jnp.where(tail, 2 * quarter, 0), n, greet, 0)
+    for copy in small:
+        copy.start()
 
     @pl.when(me == 0)
     def _():

time: 34.4 us -> 33.8 us (0.983)
  Pallas kernels: 33.5 us -> 33 us
    pallas_call x1, Pallas kernels: 31.5 us -> 31 us  [body(): pl.pallas_call(functools.partial(kernel, n, sizes), out_shape=tuple((pltp...]
where the time goes in v7:
time: 33.8 us; the launch traced here: 33.6 us
  Pallas kernels  33 us (98%)
  between operations  0.64 us (2%)
    pallas_call x1, Pallas kernels, body(): pl.pallas_call(functools.partial(kernel, n, sizes), out_shape=tuple((pltp...  31 us
    pallas_call x1, Pallas kernels, body(): pl.pallas_call(functools.partial(flush, n, sizes), out_shape=tuple((jax.S...  1.97 us

profile of v7, /device:TPU:0, one launch (start us, length us, event | category | flops | bytes accessed | tf_op | source)
XLA Modules:
  0.0 33.6 jit_solution(13829044733016278296)
XLA Ops:
  0.6 31.0 %shard_map.104 = (bf16[3,1024,512]{2,1,0:T(8,128)(2,1)S(1)}, bf16[3,1024,128]{2,1,0:T(8,128)(2,1)S(1)}, bf16[8,4,128,128]{3,2,1,0:T(8,128)(2,1)S(1)}, bf16[1024,...) custom-call(s32[4,8]{1,0:T(4,128)} %bitcast.5, ...), custom_call_target="tpu_custom_call" | custom-call | tf_op jit(solution)/shard_map/pallas_call | solution.py:390
  31.6 2.0 %shard_map.105 = (bf16[3,1024,512]{2,1,0:T(8,128)(2,1)}, bf16[3,1024,128]{2,1,0:T(8,128)(2,1)}) custom-call(bf16[3,1024,512]{2,1,0:T(8,128)(2,1)S(1)} %get-tuple-element.10.held_f, bf16[3,1024,128]{2,1,0:T(8,128)(2,1)S(1)} %get-tuple-element.11.held_e, bf16[8,4,128,128]{3,2,1,0:T(8,128)(2,1)S(1)} %get-tuple-element.12.tiles, ...), custom_call_target="tpu_custom_call" | custom-call | tf_op jit(solution)/shard_map/pallas_call | solution.py:431

commit v8 on v7

--- a/solution.py
+++ b/solution.py
@@ -41,6 +41,8 @@
     per = tile // 16
     pairs = HOPS * chunks
     scratch = list(scratch)
+    counted = scratch.pop(0)
+    rim_units = send_most * tile // hub_dev
     take = lambda count: [scratch.pop(0) for _ in range(count)]
     locals_, groups, sends, hub_sends = (take(pairs) for _ in range(4))
     exts = take(pairs - 1) + [last_ext]
@@ -48,7 +50,7 @@
     (
         cols_ref, listed_ref, count_ref, hubs_ref,
         features, embeddings, weight_t, degree,
-        load_sem, rim_send_sem, rim_recv_sem, hub_send_sem, hub_recv_sem, pass_sem,
+        load_sem, send_sem, recv_sem, pass_sem,
     ) = scratch
     me = lax.axis_index("dom")
 
@@ -111,37 +113,34 @@
         return pltpu.make_async_remote_copy(
             src_ref=sends[i].at[side],
             dst_ref=exts[i].at[pl.ds(first, send_most)],
-            send_sem=rim_send_sem.at[i % chunks],
-            recv_sem=rim_recv_sem.at[i % (2 * chunks)],
+            send_sem=send_sem.at[i % chunks],
+            recv_sem=recv_sem.at[i % (2 * chunks)],
             device_id=(to,),
             device_id_type=MESH,
         )
 
+    even = lax.rem(me, 2) == 0
     inner = jnp.logical_and(me > 0, me < n - 1)
 
-    def rim_wait(i, sem):
-        def of(count):
-            some = exts[i].at[pl.ds(blocks, count)]
-            return pltpu.make_async_copy(some, some, sem)
-
+    def wait_for(units, sem):
+        some = counted.at[pl.ds(0, units)]
+        pltpu.make_async_copy(some, some, sem).wait()
+
+    def joint_wait(hub_rows, sem):
         @pl.when(inner)
         def _():
-            of(2 * send_most).wait()
+            wait_for(hub_rows + 2 * rim_units, sem)
 
         @pl.when(jnp.logical_not(inner))
         def _():
-            of(send_most).wait()
-
-    def hub_wait(i, sem, count=n - 1):
-        some = hub_bufs[i].at[pl.ds(0, count)]
-        pltpu.make_async_copy(some, some, sem).wait()
-
-    def hub_copy(i, held, owner, to, recv_sem):
+            wait_for(hub_rows + rim_units, sem)
+
+    def hub_copy(i, held, owner, to, sem):
         return pltpu.make_async_remote_copy(
             src_ref=held,
             dst_ref=hub_bufs[i].at[owner],
-            send_sem=hub_send_sem.at[i % chunks],
-            recv_sem=recv_sem,
+            send_sem=send_sem.at[i % chunks],
+            recv_sem=sem,
             device_id=(to,),
             device_id_type=MESH,
         )
@@ -165,7 +164,7 @@
         hub_bufs[i][me] = packed
 
     def launch_rims(i):
-        @pl.when(me < n - 1)
+        @pl.when(even)
         def _():
             rim_copy(i, 1).start()
 
@@ -173,20 +172,24 @@
         def _():
             rim_copy(i, 0).start()
 
+        @pl.when(jnp.logical_and(jnp.logical_not(even), me < n - 1))
+        def _():
+            rim_copy(i, 1).start()
+
     def launch_hubs(i):
-        recv_sem = hub_recv_sem.at[i % (2 * chunks)]
+        joint = recv_sem.at[i % (2 * chunks)]
 
         def spread(step, carry):
-            hub_copy(i, hub_sends[i], me, lax.rem(me + step, n), recv_sem).start()
+            hub_copy(i, hub_sends[i], me, lax.rem(me + step, n), joint).start()
             return carry
 
         lax.fori_loop(1, n, spread, 0)
 
     def launch_first(c):
-        recv_sem = hub_recv_sem.at[c]
+        joint = recv_sem.at[c]
 
         def spread(step, carry):
-            hub_copy(c, hub_sends[c], me, lax.rem(me + step, n), recv_sem).start()
+            hub_copy(c, hub_sends[c], me, lax.rem(me + step, n), joint).start()
             return carry
 
         @pl.when(head)
@@ -200,7 +203,7 @@
 
                 @pl.when(to != passer)
                 def _():
-                    hub_copy(c, hub_sends[c], me, to, recv_sem).start()
+                    hub_copy(c, hub_sends[c], me, to, joint).start()
 
                 return carry
 
@@ -212,27 +215,21 @@
 
     def pass_on(c, source):
         owner = me - (2 - source) * quarter
-        hub_wait(c, pass_sem.at[c, source], 1)
+        wait_for(1, pass_sem.at[c, source])
 
         def spread(step, carry):
             to = 3 * quarter + lax.rem(me + step, quarter)
-            hub_copy(c, hub_bufs[c].at[owner], owner, to, hub_recv_sem.at[c]).start()
+            hub_copy(c, hub_bufs[c].at[owner], owner, to, recv_sem.at[c]).start()
             return carry
 
         lax.fori_loop(0, quarter, spread, 0)
 
-    def first_wait(c, sem, of_head, of_third):
-        @pl.when(head)
-        def _():
-            hub_wait(c, sem, of_head)
-
-        @pl.when(third)
-        def _():
-            hub_wait(c, sem, of_third)
-
-        @pl.when(tail)
-        def _():
-            hub_wait(c, sem)
+    def first_wait(sem, of_head, of_third):
+        for group, hub_rows in ((head, of_head), (third, of_third), (tail, n - 1)):
+
+            @pl.when(group)
+            def _(hub_rows=hub_rows):
+                joint_wait(hub_rows, sem)
 
     def prepare(c):
         which, at, width = pieces[c]
@@ -283,16 +280,13 @@
             which, at, width = pieces[c]
             with jax.named_scope(f"hubwait_{hop}_{c}"):
                 if hop:
-                    hub_wait(i, hub_recv_sem.at[i % (2 * chunks)])
+                    joint_wait(n - 1, recv_sem.at[i % (2 * chunks)])
                 else:
-                    first_wait(c, hub_recv_sem.at[c], n - 1, n - 3)
-            with jax.named_scope(f"rimwait_{hop}_{c}"):
-                rim_wait(i, rim_recv_sem.at[i % (2 * chunks)])
-
+                    first_wait(recv_sem.at[c], n - 1, n - 3)
             if i == pairs - 1:
                 continue
 
-            hubs = hub_bufs[i][:n].reshape(n * hub_dev, width)
+            hubs = hub_bufs[i][...].reshape(n * hub_dev, width)
 
             def one(b, carry):
                 rows = pl.ds(pl.multiple_of(b * tile, tile), tile)
@@ -313,18 +307,16 @@
                 with jax.named_scope(f"launch_{hop}_{c}"):
                     stage_hubs(j)
                     if hop:
-                        hub_wait(i, hub_send_sem.at[c])
+                        joint_wait(n - 1, send_sem.at[c])
                     else:
-                        first_wait(c, hub_send_sem.at[c], n - 1 - quarter, n - 1 + 2 * quarter)
+                        first_wait(send_sem.at[c], n - 1 - quarter, n - 1 + 2 * quarter)
                     launch_hubs(j)
                     stage_rims(j)
-                    rim_wait(i, rim_send_sem.at[c])
                     launch_rims(j)
 
     with jax.named_scope("drain"):
         for i in range(pairs - chunks, pairs):
-            hub_wait(i, hub_send_sem.at[i % chunks])
-            rim_wait(i, rim_send_sem.at[i % chunks])
+            joint_wait(n - 1, send_sem.at[i % chunks])
 
 
 def flush(
@@ -346,7 +338,7 @@
     for copy in copies:
         copy.start()
     fetch.wait()
-    hubs = hubs_ref[:n].reshape(n * hub_dev, width)
+    hubs = hubs_ref[...].reshape(n * hub_dev, width)
 
     def one(b, carry):
         rows = pl.ds(pl.multiple_of(b * tile, tile), tile)
@@ -373,6 +365,8 @@
     pieces = cut(0, features.shape[1]) + cut(1, embeddings.shape[1])
     sizes = (blocks, tile, taps, send_most, hub_dev, pieces)
     widths = [width for _, _, width in pieces] * HOPS
+    assert set(widths) == {WIDTH}
+    units = 2 * send_most * tile // hub_dev
     vmem = pl.BlockSpec(memory_space=pltpu.VMEM)
     hbm = pl.BlockSpec(memory_space=pltpu.HBM)
     bf16 = jnp.bfloat16
@@ -383,7 +377,7 @@
         ((rows, n * hub_dev), bf16),
         ((blocks, tile, LANES), jnp.float32),
         ((blocks + 2 * send_most, tile, widths[-1]), bf16),
-        ((n + n // 2, hub_dev, widths[-1]), bf16),
+        ((n, hub_dev, widths[-1]), bf16),
         ((taps, blocks), jnp.int32),
     ]
     out_bytes = sum(math.prod(shape[:-1]) * max(shape[-1], LANES) * jnp.dtype(kind).itemsize for shape, kind in results)
@@ -392,7 +386,8 @@
         out_shape=tuple(pltpu.VMEM(shape, kind) for shape, kind in results),
         in_specs=[hbm] * 9,
         out_specs=(vmem,) * len(results),
-        scratch_shapes=[
+        scratch_shapes=[pltpu.VMEM((n + n // 2 + units, hub_dev, WIDTH), bf16)]
+        + [
             pltpu.VMEM(shape + (width,), bf16)
             for shape, some in (
                 ((blocks, tile), widths),
@@ -400,7 +395,7 @@
                 ((2, send_most, tile), widths),
                 ((hub_dev,), widths),
                 ((blocks + 2 * send_most, tile), widths[:-1]),
-                ((n + n // 2, hub_dev), widths[:-1]),
+                ((n, hub_dev), widths[:-1]),
             )
             for width in some
         ]
@@ -414,8 +409,6 @@
             pltpu.VMEM((n * hub_dev, rows), bf16),
             pltpu.VMEM((blocks, tile), jnp.int32),
             pltpu.SemaphoreType.DMA((6,)),
-            pltpu.SemaphoreType.DMA((len(pieces),)),
-            pltpu.SemaphoreType.DMA((2 * len(pieces),)),
             pltpu.SemaphoreType.DMA((len(pieces),)),
             pltpu.SemaphoreType.DMA((2 * len(pieces),)),
             pltpu.SemaphoreType.DMA((len(pieces), 2)),

time: 33.8 us -> 33.7 us (level)
  no operation moved by 1% of the time
where the time goes in v8:
time: 33.7 us; the launch traced here: 33.5 us
  Pallas kernels  32.8 us (97%)
  between operations  0.64 us (2%)
    pallas_call x1, Pallas kernels, body(): pl.pallas_call(functools.partial(kernel, n, sizes), out_shape=tuple((pltp...  30.9 us
    pallas_call x1, Pallas kernels, body(): pl.pallas_call(functools.partial(flush, n, sizes), out_shape=tuple((jax.S...  1.97 us

profile of v8, /device:TPU:0, one launch (start us, length us, event | category | flops | bytes accessed | tf_op | source)
XLA Modules:
  0.0 33.5 jit_solution(10389168912326486452)
XLA Ops:
  0.6 30.9 %shard_map.104 = (bf16[3,1024,512]{2,1,0:T(8,128)(2,1)S(1)}, bf16[3,1024,128]{2,1,0:T(8,128)(2,1)S(1)}, bf16[8,4,128,128]{3,2,1,0:T(8,128)(2,1)S(1)}, bf16[1024,...) custom-call(s32[4,8]{1,0:T(4,128)} %bitcast.5, ...), custom_call_target="tpu_custom_call" | custom-call | tf_op jit(solution)/shard_map/pallas_call | solution.py:384
  31.5 2.0 %shard_map.105 = (bf16[3,1024,512]{2,1,0:T(8,128)(2,1)}, bf16[3,1024,128]{2,1,0:T(8,128)(2,1)}) custom-call(bf16[3,1024,512]{2,1,0:T(8,128)(2,1)S(1)} %get-tuple-element.10.held_f, bf16[3,1024,128]{2,1,0:T(8,128)(2,1)S(1)} %get-tuple-element.11.held_e, bf16[8,4,128,128]{3,2,1,0:T(8,128)(2,1)S(1)} %get-tuple-element.12.tiles, ...), custom_call_target="tpu_custom_call" | custom-call | tf_op jit(solution)/shard_map/pallas_call | solution.py:424

commit v9 on v8

--- a/solution.py
+++ b/solution.py
@@ -58,7 +58,10 @@
         return pltpu.make_async_copy(source, held, load_sem.at[q])
 
     load_degree = load(degree_hbm, degree, 0)
-    load_features = load(features_hbm, features, 1)
+    lead = pieces[0][2]
+    rest = features.shape[1] - lead
+    load_features = load(features_hbm.at[:, pl.ds(0, lead)], features.at[:, pl.ds(0, lead)], 1)
+    load_rest = load(features_hbm.at[:, pl.ds(lead, rest)], features.at[:, pl.ds(lead, rest)], 6)
     load_embeddings = load(embeddings_hbm, embeddings, 2)
     small = [
         load(listed_hbm, listed_ref, 3),
@@ -71,7 +74,7 @@
         load(cols_hbm, cols_ref, 2),
         load(cols_hbm, cols_held, 3),
     ]
-    for copy in [load_degree, load_features, load_embeddings]:
+    for copy in [load_degree, load_features, load_rest, load_embeddings]:
         copy.start()
 
     barrier = pltpu.get_barrier_semaphore()
@@ -245,12 +248,15 @@
 
         lax.fori_loop(0, blocks, one, 0, unroll=UNROLL)
 
-    for copy in small + [load_features, load_embeddings]:
+    for copy in small + [load_features]:
         copy.wait()
-    for copy in late:
-        copy.start()
 
     for c in range(chunks):
+        if c == 1:
+            load_rest.wait()
+            load_embeddings.wait()
+            for copy in late:
+                copy.start()
         with jax.named_scope("prepare"):
             prepare(c)
             stage_hubs(c)
@@ -408,7 +414,7 @@
             pltpu.VMEM(embeddings.shape, bf16),
             pltpu.VMEM((n * hub_dev, rows), bf16),
             pltpu.VMEM((blocks, tile), jnp.int32),
-            pltpu.SemaphoreType.DMA((6,)),
+            pltpu.SemaphoreType.DMA((7,)),
             pltpu.SemaphoreType.DMA((len(pieces),)),
             pltpu.SemaphoreType.DMA((2 * len(pieces),)),
             pltpu.SemaphoreType.DMA((len(pieces), 2)),

time: 33.7 us -> 33.7 us (level)
  no operation moved by 1% of the time
where the time goes in v9:
time: 33.7 us; the launch traced here: 33.5 us
  Pallas kernels  32.8 us (97%)
  between operations  0.64 us (2%)
    pallas_call x1, Pallas kernels, body(): pl.pallas_call(functools.partial(kernel, n, sizes), out_shape=tuple((pltp...  30.9 us
    pallas_call x1, Pallas kernels, body(): pl.pallas_call(functools.partial(flush, n, sizes), out_shape=tuple((jax.S...  1.97 us

profile of v9, /device:TPU:0, one launch (start us, length us, event | category | flops | bytes accessed | tf_op | source)
XLA Modules:
  0.0 33.5 jit_solution(18026116973215736093)
XLA Ops:
  0.6 30.9 %shard_map.104 = (bf16[3,1024,512]{2,1,0:T(8,128)(2,1)S(1)}, bf16[3,1024,128]{2,1,0:T(8,128)(2,1)S(1)}, bf16[8,4,128,128]{3,2,1,0:T(8,128)(2,1)S(1)}, bf16[1024,...) custom-call(s32[4,8]{1,0:T(4,128)} %bitcast.5, ...), custom_call_target="tpu_custom_call" | custom-call | tf_op jit(solution)/shard_map/pallas_call | solution.py:390
  31.5 2.0 %shard_map.105 = (bf16[3,1024,512]{2,1,0:T(8,128)(2,1)}, bf16[3,1024,128]{2,1,0:T(8,128)(2,1)}) custom-call(bf16[3,1024,512]{2,1,0:T(8,128)(2,1)S(1)} %get-tuple-element.10.held_f, bf16[3,1024,128]{2,1,0:T(8,128)(2,1)S(1)} %get-tuple-element.11.held_e, bf16[8,4,128,128]{3,2,1,0:T(8,128)(2,1)S(1)} %get-tuple-element.12.tiles, ...), custom_call_target="tpu_custom_call" | custom-call | tf_op jit(solution)/shard_map/pallas_call | solution.py:430

commit v10 on v8

--- a/solution.py
+++ b/solution.py
@@ -180,10 +180,10 @@
         joint = recv_sem.at[i % (2 * chunks)]
 
         def spread(step, carry):
-            hub_copy(i, hub_sends[i], me, lax.rem(me + step, n), joint).start()
+            hub_copy(i, hub_sends[i], me, step + (step >= me).astype(jnp.int32), joint).start()
             return carry
 
-        lax.fori_loop(1, n, spread, 0)
+        lax.fori_loop(0, n - 1, spread, 0)
 
     def launch_first(c):
         joint = recv_sem.at[c]

time: 33.7 us -> 33.7 us (level)
  no operation moved by 1% of the time
where the time goes in v10:
time: 33.7 us; the launch traced here: 33.5 us
  Pallas kernels  32.8 us (97%)
  between operations  0.64 us (2%)
    pallas_call x1, Pallas kernels, body(): pl.pallas_call(functools.partial(kernel, n, sizes), out_shape=tuple((pltp...  30.8 us
    pallas_call x1, Pallas kernels, body(): pl.pallas_call(functools.partial(flush, n, sizes), out_shape=tuple((jax.S...  1.97 us

profile of v10, /device:TPU:0, one launch (start us, length us, event | category | flops | bytes accessed | tf_op | source)
XLA Modules:
  0.0 33.5 jit_solution(17330334258612934705)
XLA Ops:
  0.6 30.8 %shard_map.104 = (bf16[3,1024,512]{2,1,0:T(8,128)(2,1)S(1)}, bf16[3,1024,128]{2,1,0:T(8,128)(2,1)S(1)}, bf16[8,4,128,128]{3,2,1,0:T(8,128)(2,1)S(1)}, bf16[1024,...) custom-call(s32[4,8]{1,0:T(4,128)} %bitcast.5, ...), custom_call_target="tpu_custom_call" | custom-call | tf_op jit(solution)/shard_map/pallas_call | solution.py:384
  31.5 2.0 %shard_map.105 = (bf16[3,1024,512]{2,1,0:T(8,128)(2,1)}, bf16[3,1024,128]{2,1,0:T(8,128)(2,1)}) custom-call(bf16[3,1024,512]{2,1,0:T(8,128)(2,1)S(1)} %get-tuple-element.10.held_f, bf16[3,1024,128]{2,1,0:T(8,128)(2,1)S(1)} %get-tuple-element.11.held_e, bf16[8,4,128,128]{3,2,1,0:T(8,128)(2,1)S(1)} %get-tuple-element.12.tiles, ...), custom_call_target="tpu_custom_call" | custom-call | tf_op jit(solution)/shard_map/pallas_call | solution.py:424
